TPU v7x, 256 devices: a whole 4x4x8 slice. The times are simulated.
256 devices in a mesh: seq: 64 (over z, y, core), head: 4 (over x).
Axes of the slice: x: 4, y: 4, z: 8, core: 2. Of those that a mesh axis runs over, the one named last changes fastest.
Arguments:
- tokens: bfloat16 [8192, 2048], P('seq'), may hold values from -20 to 20, as said below
- projection: bfloat16 [2048, 3072], P(None, 'head'), may hold values from -0.078125 to 0.078125
- context_cotangent: bfloat16 [8192, 2048], P('seq', 'head'), may hold values from -80 to 80
Outputs:
- perturbed_context: bfloat16 [8192, 2048], P('seq', 'head')
- ascent_direction: float32 [2048, 3072], P('seq', 'head')
Inputs may be any that keep to these rules, and one draw needn't show every extreme that they name: `tokens`: activations of the layer.
All inputs are finite; a program needn't handle non-finite values.
Results may differ from a plain program's by a relative error of at most 0.017.
Values may be sent and summed in bfloat16 or wider, within the bound.
No kernel may reach another device: no remote copies, remote signals or barrier semaphores. Data moves between devices by JAX's collectives and lax.ppermute only.
A program may use at most 64 MiB of HBM per device.

v0:
```python
import math
import jax
import jax.numpy as jnp
from jax import lax
from jax.sharding import Mesh
from jax.sharding import PartitionSpec as P

INPUT_FEATURES = 2048
KEY_VALUE_HEADS = 4
HEAD_DIMENSION = 128
QUERY_PER_GROUP = 4
SEQ = ("seq_0", "seq_1", "seq_2")
masked_score = -1e30
key_block = 512


def scatter_axes(shard, axes, dim):
    for axis in axes:
        shard = lax.psum_scatter(shard, axis, scatter_dimension=dim, tiled=True)
    return shard


def sent_to_all(shard, axis):
    length = lax.axis_size(axis)
    return lax.all_to_all(
        jnp.broadcast_to(shard[None], (length, *shard.shape)), axis, 0, 0, tiled=True
    )


def taken_together(shard, axis):
    everything = sent_to_all(shard, axis)
    return jnp.sum(everything, axis=0)


def joined_along(tiles, dim):
    tiles = jnp.moveaxis(tiles, 0, dim)
    dims = tiles.shape
    return tiles.reshape(*dims[:dim], dims[dim] * dims[dim + 1], *dims[dim + 2 :])


def stacked_from(shard, axes, turns):
    tiles = shard[None]
    for k in turns:
        tiles = lax.all_gather(tiles, axes[k], axis=0, tiled=True)
    carried = [lax.axis_size(axes[k]) for k in reversed(turns)]
    tiles = tiles.reshape(*carried, *shard.shape)
    turned = sorted(range(len(turns)), key=lambda place: turns[len(turns) - 1 - place])
    return tiles.transpose(*turned, *range(len(turns), tiles.ndim)).reshape(-1, *shard.shape)


def gathered_by_axis(shard, axes, turns, dim):
    return joined_along(stacked_from(shard, axes, turns), dim)


def attend_fold(query_rows, query_pos, score_scale):
    head_size = query_rows.shape[1]

    def single_block(carry_state, block_rows, offset):
        running_max, row_total, context_sum = carry_state
        key_rows = block_rows[:, :head_size]
        value_rows = block_rows[:, head_size:].astype(jnp.float32)
        scores = jnp.dot(query_rows, key_rows.T, preferred_element_type=jnp.float32) * score_scale
        key_pos = offset + jnp.arange(block_rows.shape[0], dtype=jnp.int32)
        allowed = key_pos[None, :] <= query_pos[:, None]
        scores = jnp.where(allowed, scores, masked_score)
        new_max = jnp.maximum(running_max, jnp.max(scores, axis=1))
        factor = jnp.exp(running_max - new_max)
        weights = jnp.where(allowed, jnp.exp(scores - new_max[:, None]), 0.0)
        row_total = row_total * factor + jnp.sum(weights, axis=1)
        context_sum = context_sum * factor[:, None] + jnp.dot(
            weights, value_rows, preferred_element_type=jnp.float32
        )
        return (new_max, row_total, context_sum)

    def fold_keys(carry_state, block_rows, offset):
        row_count = block_rows.shape[0]
        if row_count > key_block and row_count % key_block == 0:

            def sub_block(block_index, inner_state):
                part_rows = lax.dynamic_slice_in_dim(
                    block_rows, block_index * key_block, key_block, 0
                )
                return single_block(inner_state, part_rows, block_index * key_block)

            return lax.fori_loop(0, row_count // key_block, sub_block, carry_state)
        return single_block(carry_state, block_rows, offset)

    return fold_keys


def on_device(tokens, projection, context_cotangent):
    score_scale = HEAD_DIMENSION ** (-0.5)
    local_rows = tokens.shape[0]
    rows_all = local_rows * QUERY_PER_GROUP
    first_row = lax.axis_index(SEQ) * local_rows
    query_pos = first_row + jnp.arange(rows_all, dtype=jnp.int32) // QUERY_PER_GROUP

    def split_heads(projected_weight):
        reshaped_grads = projected_weight.reshape(local_rows, QUERY_PER_GROUP + 2, HEAD_DIMENSION)
        query_rows = reshaped_grads[:, :QUERY_PER_GROUP].reshape(rows_all, HEAD_DIMENSION)
        key_value = reshaped_grads[:, QUERY_PER_GROUP:].reshape(local_rows, 2 * HEAD_DIMENSION)
        return (query_rows, key_value)

    def empty_state():
        return (
            jnp.full((rows_all,), masked_score, jnp.float32),
            jnp.zeros((rows_all,), jnp.float32),
            jnp.zeros((rows_all, HEAD_DIMENSION), jnp.float32),
        )

    projected_weight = jnp.dot(tokens, projection, preferred_element_type=jnp.float32).astype(
        jnp.bfloat16
    )
    query_rows, key_value = split_heads(projected_weight)
    gathered = lax.all_gather(key_value, SEQ, axis=0, tiled=True)
    total_rows = gathered.shape[0]
    block_size = min(key_block, total_rows)
    needed = (first_row + local_rows - 1) // block_size + 1
    fold_first = attend_fold(query_rows, query_pos, score_scale)

    def forward_step(block_index, carry_state):
        block_rows = lax.dynamic_slice_in_dim(gathered, block_index * block_size, block_size, 0)
        return fold_first(carry_state, block_rows, block_index * block_size)

    running_max, row_total, context_sum = lax.fori_loop(0, needed, forward_step, empty_state())
    context = (context_sum / row_total[:, None]).astype(jnp.bfloat16)
    log_total = running_max + jnp.log(row_total)
    grad_rows = context_cotangent.reshape(rows_all, HEAD_DIMENSION)
    row_delta = jnp.sum(grad_rows.astype(jnp.float32) * context.astype(jnp.float32), axis=1)
    contract_rows = (((0,), (0,)), ((), ()))

    def backward_step(block_index, carry_state):
        query_grad, key_terms = carry_state
        offset = block_index * block_size
        block_rows = lax.dynamic_slice_in_dim(gathered, offset, block_size, 0)
        key_rows = block_rows[:, :HEAD_DIMENSION]
        value_rows = block_rows[:, HEAD_DIMENSION:]
        scores = jnp.dot(query_rows, key_rows.T, preferred_element_type=jnp.float32) * score_scale
        key_pos = offset + jnp.arange(block_size, dtype=jnp.int32)
        allowed = key_pos[None, :] <= query_pos[:, None]
        probs_full = jnp.where(allowed, jnp.exp(scores - log_total[:, None]), 0.0)
        probs_half = probs_full.astype(jnp.bfloat16)
        prob_grad = jnp.dot(grad_rows, value_rows.T, preferred_element_type=jnp.float32)
        score_grad = (probs_full * (prob_grad - row_delta[:, None]) * score_scale).astype(
            jnp.bfloat16
        )
        query_grad = query_grad + jnp.dot(score_grad, key_rows, preferred_element_type=jnp.float32)
        key_grad = lax.dot_general(
            score_grad, query_rows, contract_rows, preferred_element_type=jnp.float32
        )
        value_grad = lax.dot_general(
            probs_half, grad_rows, contract_rows, preferred_element_type=jnp.float32
        )
        key_terms = lax.dynamic_update_slice_in_dim(
            key_terms, jnp.concatenate([key_grad, value_grad], axis=1), offset, 0
        )
        return (query_grad, key_terms)

    initial = (
        jnp.zeros((rows_all, HEAD_DIMENSION), jnp.float32),
        jnp.zeros((total_rows, 2 * HEAD_DIMENSION), jnp.float32),
    )
    query_grad, key_terms = lax.fori_loop(0, needed, backward_step, initial)
    key_value_grad = scatter_axes(key_terms, SEQ, 0).astype(jnp.bfloat16)
    head_grads = jnp.concatenate(
        [
            query_grad.astype(jnp.bfloat16).reshape(local_rows, QUERY_PER_GROUP * HEAD_DIMENSION),
            key_value_grad,
        ],
        axis=1,
    )
    grad_term = lax.dot_general(
        tokens, head_grads, contract_rows, preferred_element_type=jnp.float32
    )
    normalizing_scale = math.sqrt(
        INPUT_FEATURES * KEY_VALUE_HEADS * (QUERY_PER_GROUP + 2) * HEAD_DIMENSION
    )
    ascent_radius = 0.2 * math.sqrt(KEY_VALUE_HEADS * (QUERY_PER_GROUP + 2) * HEAD_DIMENSION)
    weight_grad = lax.psum(grad_term, SEQ)
    square_sum = taken_together(jnp.sum(weight_grad * weight_grad), "head")
    grad_norm = jnp.sqrt(square_sum)
    share_rows = INPUT_FEATURES // lax.axis_size(SEQ)
    own_grad = lax.dynamic_slice_in_dim(
        weight_grad, lax.axis_index(SEQ) * share_rows, share_rows, 0
    )
    direction = own_grad * (normalizing_scale / grad_norm)
    moved_weights = (
        projection.astype(jnp.float32) + ascent_radius / grad_norm * weight_grad
    ).astype(jnp.bfloat16)
    projected_new = jnp.dot(tokens, moved_weights, preferred_element_type=jnp.float32).astype(
        jnp.bfloat16
    )
    query_new, key_value_new = split_heads(projected_new)
    fold_new = attend_fold(query_new, query_pos, score_scale)
    final_state = fold_new(
        empty_state(), gathered_by_axis(key_value_new, SEQ, (1, 0, 2), 0), jnp.int32(0)
    )
    perturbed = (
        (final_state[2] / final_state[1][:, None])
        .astype(jnp.bfloat16)
        .reshape(local_rows, QUERY_PER_GROUP * HEAD_DIMENSION)
    )
    return (perturbed, direction)


def solution(mesh):
    finer = Mesh(
        mesh.devices.reshape(8, 4, 2, mesh.shape["head"]), ("seq_0", "seq_1", "seq_2", "head")
    )
    placed = (P(SEQ, None), P(None, "head"), P(SEQ, "head"))
    return jax.shard_map(
        on_device,
        mesh=finer,
        in_specs=placed,
        out_specs=(P(SEQ, "head"), P(SEQ, "head")),
        check_vma=False,
    )
```

profile of v0, /device:TPU:1, one launch (start us, length us, event | category | flops | bytes accessed | tf_op | source)
XLA Modules:
  0.0 723.9 jit_solution(13365416468607866390)
XLA Ops:
  8.2 2.5 convolution_convert_fusion
  12.0 83.2 %all-gather.4.cloned.1.call-done = bf16[8192,256]{1,0:T(8,128)(2,1)} async-done(((bf16[128,256]{1,0:T(8,128)(2,1)}), bf16[8192,256]{1,0:T(8,128)(2,1)}) %all-gather.4.cloned.1.call-update) | async-done | bytes 4194320 | tf_op jit(solution)/shard_map/all_gather | solution.py:115
  95.2 3.0 while.46
  96.8 1.4 convolution_add_fusion.6
  98.5 4.2 broadcast_in_dim.56
  102.7 5.3 while.47
  108.1 214.4 %reduce-scatter.4.cloned.1.call-done = f32[1024,256]{0,1:T(8,128)} async-done(((f32[8192,256]{0,1:T(8,128)}), f32[1024,256]{0,1:T(8,128)}) %reduce-scatter.4.cloned.1.call-update) | async-done | bytes 1048592 | tf_op jit(solution)/shard_map/reduce_scatter | solution.py:19
  322.6 26.0 %reduce-scatter.6.cloned.1.call-done = f32[256,256]{0,1:T(8,128)} async-done(((f32[1024,256]{0,1:T(8,128)}), f32[256,256]{0,1:T(8,128)}) %reduce-scatter.6.cloned.1.call-update) | async-done | bytes 262160 | tf_op jit(solution)/shard_map/reduce_scatter | solution.py:19
  348.8 17.3 %reduce-scatter.8.cloned.1.call-done = f32[128,256]{0,1:T(8,128)} async-done(((f32[256,256]{0,1:T(8,128)}), f32[128,256]{0,1:T(8,128)}) %reduce-scatter.8.cloned.1.call-update) | async-done | bytes 131088 | tf_op jit(solution)/shard_map/reduce_scatter | solution.py:19
  367.1 3.7 convolution_bitcast_fusion
  370.8 4.7 copy.49
  375.5 195.1 %all-reduce.2.cloned.1.call-done = f32[2048,768]{0,1:T(8,128)} async-done(((f32[2048,768]{0,1:T(8,128)}), f32[2048,768]{0,1:T(8,128)}) %all-reduce.2.cloned.1.call-update) | async-done | bytes 6291472 | tf_op jit(solution)/shard_map/psum | solution.py:179
  570.6 5.0 multiply_reduce_fusion
  576.3 7.9 %all_to_all.6 = f32[4,1,1]{2,1,0:T(1,128)S(1)} all-to-all(f32[4,1,1]{2,1,0:T(1,128)S(1)} %broadcast_in_dim.57), channel_id=1, replica_groups=mesh['seq_0'=8,'seq_1'=4,'seq_2'=2,'head'=4] {'head'}, dimensions={0} | all-to-all | bytes 32 | tf_op jit(solution)/shard_map/all_to_all | solution.py:25
  585.5 4.7 fusion.58
  590.4 10.1 %all_gather.13 = bf16[4,128,256]{2,1,0:T(8,128)(2,1)} all-gather(bf16[1,128,256]{2,1,0:T(8,128)(2,1)S(1)} %copy.59), channel_id=1, replica_groups=mesh['seq_0'=8,'seq_1'=4,'seq_2'=2,'head'=4] {'seq_1'}, dimensions={0}, use_global_device_ids=true | all-gather | bytes 327680 | tf_op jit(solution)/shard_map/all_gather | solution.py:44
  600.6 39.3 %all-gather.6.cloned.1.call-done = bf16[32,128,256]{2,1,0:T(8,128)(2,1)} async-done(((bf16[4,128,256]{2,1,0:T(8,128)(2,1)}), bf16[32,128,256]{2,1,0:T(8,128)(2,1)}) %all-gather.6.cloned.1.call-update) | async-done | bytes 2097168 | tf_op jit(solution)/shard_map/all_gather | solution.py:44
  642.1 22.1 %all-gather.8.cloned.1.call-done = bf16[64,128,256]{2,1,0:T(8,128)(2,1)} async-done(((bf16[32,128,256]{2,1,0:T(8,128)(2,1)}), bf16[64,128,256]{2,1,0:T(8,128)(2,1)}) %all-gather.8.cloned.1.call-update) | async-done | bytes 4194320 | tf_op jit(solution)/shard_map/all_gather | solution.py:44
  664.2 4.6 copy.56
  668.8 47.4 %while.48 = (s32[]{:T(128)}, f32[512]{0:T(512)S(1)}, f32[512]{0:T(512)S(1)}, f32[512,128]{1,0:T(8,128)S(1)}, bf16[8192,256]{1,0:T(8,128)(2,1)}, /*index=5*/bf16[...) while((s32[]{:T(128)}, f32[512]{0:T(512)S(1)}, ...), condition=%wide.region_16.17_spmd.clone, body=%wide.region_13.16_spmd.clone.sunk | while | flops 137305600 | bytes 4112599 | solution.py:85
  670.3 1.4 convolution_add_fusion.8
  676.2 1.4 convolution_add_fusion.8
  682.2 1.4 convolution_add_fusion.8
  685.1 1.4 convolution_add_fusion.8
  (168 shorter events, 55.9 us)
Async XLA Ops:
  7.2 1.0 copy-start
  7.2 4.7 copy-start.1
  7.2 88.0 %all-gather.4.cloned.1.call-start = ((), (), s32[]{:S(2)}) async-start(), calls=%async_computation.4 | async-start | bytes 4259840 | tf_op jit(solution)/shard_map/all_gather | solution.py:115
  11.6 310.9 %reduce-scatter.4.cloned.1.call-start = ((), (), s32[]{:S(2)}) async-start(), calls=%async_computation.5 | async-start | bytes 9437184 | tf_op jit(solution)/shard_map/reduce_scatter | solution.py:19
  108.0 240.5 %reduce-scatter.6.cloned.1.call-start = ((), (), s32[]{:S(2)}) async-start(), calls=%async_computation.6 | async-start | bytes 1310720 | tf_op jit(solution)/shard_map/reduce_scatter | solution.py:19
  322.5 43.5 %reduce-scatter.8.cloned.1.call-start = ((), (), s32[]{:S(2)}) async-start(), calls=%async_computation.7 | async-start | bytes 393216 | tf_op jit(solution)/shard_map/reduce_scatter | solution.py:19
  348.6 222.0 %all-reduce.2.cloned.1.call-start = ((), (), s32[]{:S(2)}) async-start(), calls=%async_computation.8 | async-start | bytes 12582912 | tf_op jit(solution)/shard_map/psum | solution.py:179
  370.8 269.1 %all-gather.6.cloned.1.call-start = ((), (), s32[]{:S(2)}) async-start(), calls=%async_computation.9 | async-start | bytes 2359296 | tf_op jit(solution)/shard_map/all_gather | solution.py:44
  600.5 63.6 %all-gather.8.cloned.1.call-start = ((), (), s32[]{:S(2)}) async-start(), calls=%async_computation.10 | async-start | bytes 6291456 | tf_op jit(solution)/shard_map/all_gather | solution.py:44
Sparse Core Ops, SparseCore 0:
  11.8 83.3 all-gather.3
  108.2 214.2 reduce-scatter.3
  325.0 23.4 reduce-scatter.5
  350.9 15.0 reduce-scatter.7
  370.9 199.6 all-reduce.1
  600.6 39.1 all-gather.5
  641.7 22.4 all-gather.7
where the time goes:
time: 726 us; the launch traced here: 724 us
  waiting for transfers between devices  598 us (82%)
  matrix products  60.1 us (8%)
  local copies, waits for them, and re-layouts  18.4 us (3%)
  blocking collectives  18 us (2%)
  between operations  15.1 us (2%)
  other arithmetic  13.5 us (2%)
    reduce_scatter x3, waiting for transfers between devices, scatter_axes(): shard = lax.psum_scatter(shard, axis, scatter_dimension=dim, tiled=True)  258 us
    psum x1, waiting for transfers between devices, on_device(): weight_grad = lax.psum(grad_term, SEQ)  195 us
    all_gather x1, waiting for transfers between devices, on_device(): gathered = lax.all_gather(key_value, SEQ, axis=0, tiled=True)  83.2 us
    all_gather x2, waiting for transfers between devices, stacked_from(): tiles = lax.all_gather(tiles, axes[k], axis=0, tiled=True)  61.4 us
    dot_general x17, matrix products, single_block(): jnp.dot(weights, value_rows, preferred_element_type=jnp.float32)  23.9 us
    dot_general x17, matrix products, single_block(): jnp.dot(query_rows, key_rows.T, preferred_element_type=jnp.float32)  20.9 us
  transfers between devices with their start and end apart: 7, of which 7 were waited for; matrix products, arithmetic and copies ran while one was open for 1% of the time, Pallas kernels for 0%

commit v1 on v0

--- a/solution.py
+++ b/solution.py
@@ -112,7 +112,9 @@
         jnp.bfloat16
     )
     query_rows, key_value = split_heads(projected_weight)
-    gathered = lax.all_gather(key_value, SEQ, axis=0, tiled=True)
+    gathered = jnp.concatenate(
+        lax.all_to_all(jnp.stack([key_value] * lax.axis_size(SEQ)), SEQ, 0, 0), axis=0
+    )
     total_rows = gathered.shape[0]
     block_size = min(key_block, total_rows)
     needed = (first_row + local_rows - 1) // block_size + 1

time: 726 us -> 754 us (1.039)
  starting transfers between devices: 0.28 us -> 13.7 us
  waiting for transfers between devices: 598 us -> 609 us
    all_to_all x0 -> x1, waiting for transfers between devices: none -> 94.4 us  [on_device(): lax.all_to_all(jnp.stack([key_value] * lax.axis_size(SEQ)), SEQ, 0, 0)]
    all_gather x1 -> x0, waiting for transfers between devices: 83.2 us -> none  [on_device(): gathered = lax.all_gather(key_value, SEQ, axis=0, tiled=True)]
    all_to_all x0 -> x1, starting transfers between devices: none -> 13.5 us  [on_device(): lax.all_to_all(jnp.stack([key_value] * lax.axis_size(SEQ)), SEQ, 0, 0)]
where the time goes in v1:
time: 754 us; the launch traced here: 751 us
  waiting for transfers between devices  609 us (81%)
  matrix products  60.2 us (8%)
  local copies, waits for them, and re-layouts  20.2 us (3%)
  blocking collectives  18 us (2%)
  between operations  15.1 us (2%)
  starting transfers between devices  13.7 us (2%)
  other arithmetic  13.5 us (2%)
    reduce_scatter x3, waiting for transfers between devices, scatter_axes(): shard = lax.psum_scatter(shard, axis, scatter_dimension=dim, tiled=True)  258 us
    psum x1, waiting for transfers between devices, on_device(): weight_grad = lax.psum(grad_term, SEQ)  195 us
    all_to_all x1, waiting for transfers between devices, on_device(): lax.all_to_all(jnp.stack([key_value] * lax.axis_size(SEQ)), SEQ, 0, 0)  94.4 us
    all_gather x2, waiting for transfers between devices, stacked_from(): tiles = lax.all_gather(tiles, axes[k], axis=0, tiled=True)  61.2 us
    dot_general x17, matrix products, single_block(): jnp.dot(weights, value_rows, preferred_element_type=jnp.float32)  24 us
    dot_general x17, matrix products, single_block(): jnp.dot(query_rows, key_rows.T, preferred_element_type=jnp.float32)  21 us
  transfers between devices with their start and end apart: 7, of which 7 were waited for; matrix products, arithmetic and copies ran while one was open for 1% of the time, Pallas kernels for 0%

profile of v1, /device:TPU:1, one launch (start us, length us, event | category | flops | bytes accessed | tf_op | source)
XLA Modules:
  0.0 751.0 jit_solution(2494257350102554718)
XLA Ops:
  8.2 2.5 convolution_convert_fusion
  11.0 2.4 stack.3
  13.4 13.5 %all-to-all-start = ((bf16[64,128,256]{2,1,0:T(8,128)(2,1)}), bf16[64,128,256]{2,1,0:T(8,128)(2,1)}, u32[]{:S(2)}, u32[]{:S(2)}) async-start(bf16[64,128,256]{2,1,0:T(8,128)(2,1)} %stack.3), calls=%async_computation | async-start | bytes 8388608 | tf_op jit(solution)/shard_map/all_to_all | solution.py:116
  27.2 94.4 %all-to-all-done = bf16[64,128,256]{2,1,0:T(8,128)(2,1)} async-done(((bf16[64,128,256]{2,1,0:T(8,128)(2,1)}), bf16[64,128,256]{2,1,0:T(8,128)(2,1)}, u32[]{:S(2)}, u32[]{:S(2)}) %all-to-all-start) | async-done | bytes 4194336 | tf_op jit(solution)/shard_map/all_to_all | solution.py:116
  121.6 3.0 while.46
  123.2 1.4 convolution_add_fusion.6
  124.9 4.2 broadcast_in_dim.56
  129.1 5.3 while.47
  134.5 215.0 %reduce-scatter.4.cloned.1.call-done = f32[1024,256]{0,1:T(8,128)} async-done(((f32[8192,256]{0,1:T(8,128)}), f32[1024,256]{0,1:T(8,128)}) %reduce-scatter.4.cloned.1.call-update) | async-done | bytes 1048592 | tf_op jit(solution)/shard_map/reduce_scatter | solution.py:19
  349.6 26.0 %reduce-scatter.6.cloned.1.call-done = f32[256,256]{0,1:T(8,128)} async-done(((f32[1024,256]{0,1:T(8,128)}), f32[256,256]{0,1:T(8,128)}) %reduce-scatter.6.cloned.1.call-update) | async-done | bytes 262160 | tf_op jit(solution)/shard_map/reduce_scatter | solution.py:19
  375.8 17.4 %reduce-scatter.8.cloned.1.call-done = f32[128,256]{0,1:T(8,128)} async-done(((f32[256,256]{0,1:T(8,128)}), f32[128,256]{0,1:T(8,128)}) %reduce-scatter.8.cloned.1.call-update) | async-done | bytes 131088 | tf_op jit(solution)/shard_map/reduce_scatter | solution.py:19
  394.2 3.7 convolution_bitcast_fusion
  397.9 4.7 copy.49
  402.7 195.0 %all-reduce.2.cloned.1.call-done = f32[2048,768]{0,1:T(8,128)} async-done(((f32[2048,768]{0,1:T(8,128)}), f32[2048,768]{0,1:T(8,128)}) %all-reduce.2.cloned.1.call-update) | async-done | bytes 6291472 | tf_op jit(solution)/shard_map/psum | solution.py:181
  597.7 5.0 multiply_reduce_fusion
  603.4 7.9 %all_to_all.11 = f32[4,1,1]{2,1,0:T(1,128)S(1)} all-to-all(f32[4,1,1]{2,1,0:T(1,128)S(1)} %broadcast_in_dim.57), channel_id=1, replica_groups=mesh['seq_0'=8,'seq_1'=4,'seq_2'=2,'head'=4] {'head'}, dimensions={0} | all-to-all | bytes 32 | tf_op jit(solution)/shard_map/all_to_all | solution.py:25
  612.6 4.7 fusion.58
  617.5 10.1 %all_gather.9 = bf16[4,128,256]{2,1,0:T(8,128)(2,1)} all-gather(bf16[1,128,256]{2,1,0:T(8,128)(2,1)S(1)} %copy.59), channel_id=1, replica_groups=mesh['seq_0'=8,'seq_1'=4,'seq_2'=2,'head'=4] {'seq_1'}, dimensions={0}, use_global_device_ids=true | all-gather | bytes 327680 | tf_op jit(solution)/shard_map/all_gather | solution.py:44
  627.7 39.3 %all-gather.3.cloned.1.call-done = bf16[32,128,256]{2,1,0:T(8,128)(2,1)} async-done(((bf16[4,128,256]{2,1,0:T(8,128)(2,1)}), bf16[32,128,256]{2,1,0:T(8,128)(2,1)}) %all-gather.3.cloned.1.call-update) | async-done | bytes 2097168 | tf_op jit(solution)/shard_map/all_gather | solution.py:44
  669.2 21.9 %all-gather.5.cloned.1.call-done = bf16[64,128,256]{2,1,0:T(8,128)(2,1)} async-done(((bf16[32,128,256]{2,1,0:T(8,128)(2,1)}), bf16[64,128,256]{2,1,0:T(8,128)(2,1)}) %all-gather.5.cloned.1.call-update) | async-done | bytes 4194320 | tf_op jit(solution)/shard_map/all_gather | solution.py:44
  691.1 4.6 copy.56
  695.7 47.5 %while.48 = (s32[]{:T(128)}, f32[512]{0:T(512)S(1)}, f32[512]{0:T(512)S(1)}, f32[512,128]{1,0:T(8,128)S(1)}, bf16[8192,256]{1,0:T(8,128)(2,1)}, /*index=5*/bf16[...) while((s32[]{:T(128)}, f32[512]{0:T(512)S(1)}, ...), condition=%wide.region_16.17_spmd.clone, body=%wide.region_13.16_spmd.clone.sunk | while | flops 137305600 | bytes 4112599 | solution.py:85
  700.2 1.4 convolution_add_fusion.8
  706.2 1.4 convolution_add_fusion.8
  (168 shorter events, 58.2 us)
Async XLA Ops:
  7.2 1.0 copy-start
  13.4 13.7 %copy-start.1 = (bf16[128,512]{1,0:T(8,128)(2,1)S(1)}, bf16[128,512]{1,0:T(8,128)(2,1)}, u32[]{:S(2)}) copy-start(bf16[128,512]{1,0:T(8,128)(2,1)} %param.11) | copy-start | bytes 393220
  13.4 108.2 %all-to-all-start = ((bf16[64,128,256]{2,1,0:T(8,128)(2,1)}), bf16[64,128,256]{2,1,0:T(8,128)(2,1)}, u32[]{:S(2)}, u32[]{:S(2)}) async-start(bf16[64,128,256]{2,1,0:T(8,128)(2,1)} %stack.3), calls=%async_computation | async-start | bytes 8388608 | tf_op jit(solution)/shard_map/all_to_all | solution.py:116
  26.9 322.6 %reduce-scatter.4.cloned.1.call-start = ((), (), s32[]{:S(2)}) async-start(), calls=%async_computation.5 | async-start | bytes 9437184 | tf_op jit(solution)/shard_map/reduce_scatter | solution.py:19
  134.4 241.2 %reduce-scatter.6.cloned.1.call-start = ((), (), s32[]{:S(2)}) async-start(), calls=%async_computation.6 | async-start | bytes 1310720 | tf_op jit(solution)/shard_map/reduce_scatter | solution.py:19
  349.5 43.7 %reduce-scatter.8.cloned.1.call-start = ((), (), s32[]{:S(2)}) async-start(), calls=%async_computation.7 | async-start | bytes 393216 | tf_op jit(solution)/shard_map/reduce_scatter | solution.py:19
  375.6 222.1 %all-reduce.2.cloned.1.call-start = ((), (), s32[]{:S(2)}) async-start(), calls=%async_computation.8 | async-start | bytes 12582912 | tf_op jit(solution)/shard_map/psum | solution.py:181
  397.9 269.1 %all-gather.3.cloned.1.call-start = ((), (), s32[]{:S(2)}) async-start(), calls=%async_computation.9 | async-start | bytes 2359296 | tf_op jit(solution)/shard_map/all_gather | solution.py:44
  627.6 63.5 %all-gather.5.cloned.1.call-start = ((), (), s32[]{:S(2)}) async-start(), calls=%async_computation.10 | async-start | bytes 6291456 | tf_op jit(solution)/shard_map/all_gather | solution.py:44
Sparse Core Ops, SparseCore 0:
  134.6 214.8 reduce-scatter.3
  352.1 23.4 reduce-scatter.5
  378.1 15.0 reduce-scatter.7
  398.0 199.6 all-reduce.1
  627.7 39.1 all-gather.2
  668.6 22.4 all-gather.4
